TPU v7x, 32 devices: a whole 2x2x4 slice. The times are simulated.
32 devices in a mesh: seq: 8 (over z, y), chan: 4 (over x, core).
Axes of the slice: x: 2, y: 2, z: 4, core: 2. Of those that a mesh axis runs over, the one named last changes fastest.
Arguments:
- features: bfloat16 [98304, 1024], P('seq', 'chan'), may hold values from -6 to 6
- gate_input: bfloat16 [98304, 1024], P('seq', 'chan'), may hold values from -6 to 6
- input_map: bfloat16 [98304, 128], P('seq', 'chan'), may hold values from -6 to 6
- output_map: bfloat16 [98304, 128], P('seq', 'chan'), may hold values from -6 to 6
- step_raw: float32 [98304, 16], P('seq', 'chan'), may hold values from -4 to 4
- step_bias: float32 [16], P('chan')
- decay_log: float32 [16], P('chan')
- skip_gain: float32 [16], P('chan'), may hold values from 0.5 to 1.5
- norm_gain: float32 [1024], P('chan'), may hold values from 0.1 to 1.9
- tissue: int32 [192, 2], P('seq'), may hold values from 0 to 512, as said below
Outputs:
- mixed: bfloat16 [98304, 1024], P('seq', 'chan')
Inputs may be any that keep to these rules, and one draw needn't show every extreme that they name: tissue[r, 0] <= tissue[r, 1]; a row with equal values holds no tissue.
All inputs are finite; a program needn't handle non-finite values.
Results may differ from a plain program's by a relative error of at most 0.0039.
Values may be sent and summed in bfloat16 or wider, within the bound.
A program may use at most 192 MiB of HBM per device.

v0:
```python
import functools

import jax
import jax.numpy as jnp
from jax import lax
from jax.experimental import pallas as pl
from jax.experimental.pallas import tpu as pltpu
from jax.sharding import PartitionSpec as P

D = 1024
ROW = 512
EPS = 1e-05
Q = 256
HALF = 128
PAD = 8
LOG2E = 1.4426950408889634
F32 = jnp.float32
BF16 = jnp.bfloat16


def split(v, parts):
    out = []
    for _ in range(parts):
        part = lax.reduce_precision(v, 8, 7)
        out.append(part)
        v = v - part
    return out


def put_heads(xb_ref, x, heads, width):
    lane = lax.broadcasted_iota(jnp.int32, (1, HALF), 1)
    for h in range(heads):
        tile = h * width // HALF
        first = h * width - tile * HALF
        mask = ((lane >= first) & (lane < first + width)).astype(BF16)
        cols = slice(tile * HALF, (tile + 1) * HALF)
        xb_ref[h * Q : (h + 1) * Q, cols] = x[:, cols] * mask


def state_kernel(
    axis, n, heads, width, x_ref, b_ref, rows_ref, dec_ref, tot_ref, out_ref,
    xb, st, slots, send_sem, recv_sem,
):
    step = pl.program_id(0)
    last = pl.num_programs(0) - 1
    me = lax.axis_index(axis)
    states = b_ref.shape[0]

    @pl.when(step == 0)
    def _():
        barrier = pltpu.get_barrier_semaphore()
        for k in range(1, n):
            pl.semaphore_signal(barrier, inc=1, device_id={axis: lax.rem(me + k, n)})
        xb[...] = jnp.zeros_like(xb)
        st[...] = jnp.zeros_like(st)
        st[states : states + PAD, :] = jnp.broadcast_to(tot_ref[...], (PAD, st.shape[1]))

    chunks = x_ref.shape[0] // Q
    state = st[0:states, :]
    for c in range(chunks):
        at = slice(c * Q, (c + 1) * Q)
        put_heads(xb.at[c % 2], x_ref[at, :], heads, width)
        b = b_ref[:, at].astype(F32)
        coef = rows_ref[PAD : 2 * PAD, at]
        bs = jnp.concatenate(
            [(b * coef[h : h + 1, :]).astype(BF16) for h in range(heads)], axis=1
        )
        fresh = jnp.dot(bs, xb[c % 2], preferred_element_type=F32)
        state = state * dec_ref[pl.ds(step * chunks + c, 1), :] + fresh
    st[0:states, :] = state

    @pl.when(step == last)
    def _():
        barrier = pltpu.get_barrier_semaphore()
        pl.semaphore_wait(barrier, n - 1)
        copies = []
        for k in range(1, n):
            copy = pltpu.make_async_remote_copy(
                src_ref=st,
                dst_ref=slots.at[k],
                send_sem=send_sem.at[k],
                recv_sem=recv_sem.at[k],
                device_id={axis: lax.rem(me + k, n)},
            )
            copy.start()
            copies.append(copy)
        for copy in copies:
            copy.wait()
        total = jnp.zeros((states, st.shape[1]), F32)
        for k in range(n - 1, 0, -1):
            live = (k <= me).astype(F32)
            got = slots[k]
            total = total * jnp.exp2(got[states : states + 1, :] * live) + got[0:states, :] * live
        out_ref[...] = total


def band_state(x, b_all, rows, dec, tot, axis, n, heads, width):
    tokens, lanes = x.shape
    states = b_all.shape[0]
    block = 2048 if tokens % 2048 == 0 else ROW
    return pl.pallas_call(
        functools.partial(state_kernel, axis, n, heads, width),
        grid=(tokens // block,),
        in_specs=[
            pl.BlockSpec((block, lanes), lambda i: (i, 0)),
            pl.BlockSpec((states, block), lambda i: (0, i)),
            pl.BlockSpec((2 * PAD, block), lambda i: (0, i)),
            pl.BlockSpec(dec.shape, lambda i: (0, 0)),
            pl.BlockSpec((1, lanes), lambda i: (0, 0)),
        ],
        out_specs=pl.BlockSpec((states, lanes), lambda i: (0, 0)),
        out_shape=jax.ShapeDtypeStruct((states, lanes), F32),
        scratch_shapes=[
            pltpu.VMEM((2, heads * Q, lanes), BF16),
            pltpu.VMEM((states + PAD, lanes), F32),
            pltpu.VMEM((n, states + PAD, lanes), F32),
            pltpu.SemaphoreType.DMA((n,)),
            pltpu.SemaphoreType.DMA((n,)),
        ],
        compiler_params=pltpu.CompilerParams(
            collective_id=1, has_side_effects=True, vmem_limit_bytes=40 * 2**20
        ),
        cost_estimate=pl.CostEstimate(
            flops=2 * tokens * heads * states * lanes,
            bytes_accessed=tokens * (lanes + states) * 2,
            transcendentals=0,
        ),
        name="band_state",
    )(x, b_all, rows, dec, tot)


def scan_kernel(
    heads, width, x_ref, g_ref, b_ref, c_ref, rows_ref, cols_ref, sel_ref, dec_ref, in_ref,
    skip_ref, out_ref, sq_ref, lhs, xb, st,
):
    step = pl.program_id(0)
    states = b_ref.shape[0]
    lanes = x_ref.shape[1]

    @pl.when(step == 0)
    def _():
        xb[...] = jnp.zeros_like(xb)
        lhs[...] = jnp.zeros_like(lhs)
        st[...] = in_ref[...]

    chunks = x_ref.shape[0] // Q
    below = lax.broadcasted_iota(jnp.int32, (HALF, HALF), 0) >= lax.broadcasted_iota(
        jnp.int32, (HALF, HALF), 1
    )
    ones = jnp.ones((PAD, 2 * lanes), BF16)
    state = st[...]
    skip = skip_ref[...]
    for c in range(chunks):
        at = slice(c * Q, (c + 1) * Q)
        slot = c % 2
        x = x_ref[at, :]
        put_heads(xb.at[slot], x, heads, width)
        b = b_ref[:, at]
        ct = c_ref[:, at].T
        scores = jnp.dot(ct, b, preferred_element_type=F32)
        rows = rows_ref[:, at]
        wide = lax.dot_general(
            cols_ref[:, at], sel_ref[...], (((0,), (0,)), ((), ())), preferred_element_type=F32
        )
        left = slot * (Q + states)
        bf = b.astype(F32)
        for h in range(heads):
            base = h * Q
            run = wide[:, h * HALF : (h + 1) * HALF]
            near = rows[h : h + 1, 0:HALF]
            far = rows[h : h + 1, HALF:Q]
            lhs[slot, 0:HALF, base : base + HALF] = jnp.where(
                below, scores[0:HALF, 0:HALF] * jnp.exp2(run[0:HALF] - near), 0.0
            ).astype(BF16)
            lhs[slot, HALF:Q, base : base + HALF] = (
                scores[HALF:Q, 0:HALF] * jnp.exp2(run[HALF:Q] - near)
            ).astype(BF16)
            lhs[slot, HALF:Q, base + HALF : base + Q] = jnp.where(
                below, scores[HALF:Q, HALF:Q] * jnp.exp2(run[HALF:Q] - far), 0.0
            ).astype(BF16)
            lhs[slot, Q : Q + states, base : base + Q] = (
                bf * rows[PAD + h : PAD + h + 1, :]
            ).astype(BF16)
        both = jnp.dot(lhs[slot], xb[slot], preferred_element_type=F32)
        high = state.astype(BF16)
        low = (state - high.astype(F32)).astype(BF16)
        carried = jnp.dot(
            jnp.concatenate([ct, ct], axis=1),
            jnp.concatenate([high, low], axis=0),
            preferred_element_type=F32,
        )
        y = both[0:Q] + wide[:, heads * HALF :] * carried + skip * x.astype(F32)
        g = g_ref[at, :].astype(F32)
        half = 0.5 * g
        gated = y * (half + half * jnp.tanh(half))
        out_ref[at, :] = gated
        square = gated * gated
        sq_high = square.astype(BF16)
        sq_low = (square - sq_high.astype(F32)).astype(BF16)
        sq_ref[:, at] = lax.dot_general(
            ones,
            jnp.concatenate([sq_high, sq_low], axis=1),
            (((1,), (1,)), ((), ())),
            preferred_element_type=F32,
        )
        state = state * dec_ref[pl.ds(step * chunks + c, 1), :] + both[Q : Q + states]
    st[...] = state


def gated_scan(x, g, b_all, c_all, rows, cols, sel, dec, incoming, skip, heads, width):
    tokens, lanes = x.shape
    states = b_all.shape[0]
    block = 1024 if tokens % 1024 == 0 else ROW
    whole = lambda a: pl.BlockSpec(a.shape, lambda i: (0, 0))
    return pl.pallas_call(
        functools.partial(scan_kernel, heads, width),
        grid=(tokens // block,),
        in_specs=[
            pl.BlockSpec((block, lanes), lambda i: (i, 0)),
            pl.BlockSpec((block, lanes), lambda i: (i, 0)),
            pl.BlockSpec((states, block), lambda i: (0, i)),
            pl.BlockSpec((states, block), lambda i: (0, i)),
            pl.BlockSpec((2 * PAD, block), lambda i: (0, i)),
            pl.BlockSpec((cols.shape[0], block), lambda i: (0, i)),
            whole(sel),
            whole(dec),
            whole(incoming),
            whole(skip),
        ],
        out_specs=[
            pl.BlockSpec((block, lanes), lambda i: (i, 0)),
            pl.BlockSpec((PAD, block), lambda i: (0, i)),
        ],
        out_shape=[
            jax.ShapeDtypeStruct((tokens, lanes), F32),
            jax.ShapeDtypeStruct((PAD, tokens), F32),
        ],
        scratch_shapes=[
            pltpu.VMEM((2, Q + states, heads * Q), BF16),
            pltpu.VMEM((2, heads * Q, lanes), BF16),
            pltpu.VMEM((states, lanes), F32),
        ],
        compiler_params=pltpu.CompilerParams(vmem_limit_bytes=40 * 2**20),
        cost_estimate=pl.CostEstimate(
            flops=2 * tokens * heads * (Q + states) * lanes,
            bytes_accessed=tokens * (lanes * 2 + states) * 4,
            transcendentals=tokens * heads * Q,
        ),
        name="gated_scan",
    )(x, g, b_all, c_all, rows, cols, sel, dec, incoming, skip)


def per_device(
    seq_size,
    features,
    gate_input,
    input_map,
    output_map,
    step_raw,
    step_bias,
    decay_log,
    skip_gain,
    norm_gain,
    tissue,
):
    b_all = lax.all_gather(input_map.T, "chan", axis=0, tiled=True)
    c_all = lax.all_gather(output_map.T, "chan", axis=0, tiled=True)
    tokens, lanes = features.shape
    heads = step_bias.shape[0]
    width = lanes // heads
    row_count = tokens // ROW
    chunks = tokens // Q
    position = jnp.arange(ROW, dtype=jnp.int32)
    inside = ((position[None, :] >= tissue[:, 0:1]) & (position[None, :] < tissue[:, 1:2])).astype(F32)
    pad = ((0, PAD - heads), (0, 0))
    raw = step_raw.T + step_bias[:, None]
    step = jnp.pad(jax.nn.softplus(raw) * inside.reshape(1, tokens), pad)
    rate = jnp.pad(-jnp.exp(decay_log) * LOG2E, (0, PAD - heads))
    fall = (step * rate[:, None]).reshape(PAD, chunks, Q)
    upper = jnp.triu(jnp.ones((Q, Q), F32))
    running = jnp.einsum("hcs,st->hct", fall, upper, precision=lax.Precision.HIGHEST)
    total = running[:, :, -1:]
    coef = (jnp.exp2(total - running) * step.reshape(PAD, chunks, Q)).reshape(PAD, tokens)
    running = running.reshape(PAD, tokens)
    rows = jnp.concatenate([running - jnp.log2(step), coef], axis=0)
    cols = jnp.concatenate(
        split(running, 3) + split(jnp.exp2(running), 2) + [jnp.zeros_like(running)], axis=0
    ).astype(BF16)
    to_lane = jnp.repeat(jnp.eye(heads, dtype=F32), width, axis=1)
    to_half = jnp.repeat(jnp.eye(heads, dtype=F32), HALF, axis=1)
    rest = ((0, PAD - heads), (0, 0))
    to_lane, to_half = jnp.pad(to_lane, rest), jnp.pad(to_half, rest)
    sel = jnp.concatenate(
        [
            jnp.concatenate([to_half] * 3 + [jnp.zeros_like(to_half)] * 3, axis=0),
            jnp.concatenate(
                [jnp.zeros_like(to_lane)] * 3 + [to_lane] * 2 + [jnp.zeros_like(to_lane)], axis=0
            ),
        ],
        axis=1,
    ).astype(BF16)
    totals = jnp.repeat(total[:heads, :, 0].T, width, axis=1)
    dec = jnp.exp2(totals)
    band_total = jnp.sum(totals, axis=0, keepdims=True)
    incoming = band_state(
        features, b_all, rows, dec, band_total, "seq", seq_size, heads, width
    )
    skip = jnp.repeat(skip_gain, width)[None, :]
    gated, squares = gated_scan(
        features, gate_input, b_all, c_all, rows, cols, sel, dec, incoming, skip, heads, width
    )
    square_sum = lax.psum(squares[0], "chan")
    scale = lax.rsqrt(square_sum / D + EPS)
    return (gated * scale[:, None] * norm_gain).astype(BF16)


def solution(mesh):
    in_specs = (
        P("seq", "chan"),
        P("seq", "chan"),
        P("seq", "chan"),
        P("seq", "chan"),
        P("seq", "chan"),
        P("chan"),
        P("chan"),
        P("chan"),
        P("chan"),
        P("seq", None),
    )
    return jax.shard_map(
        functools.partial(per_device, mesh.shape["seq"]),
        mesh=mesh,
        in_specs=in_specs,
        out_specs=P("seq", "chan"),
        check_vma=False,
    )
```

profile of v0, /device:TPU:12, one launch (start us, length us, event | category | flops | bytes accessed | tf_op | source)
XLA Modules:
  0.0 151.1 jit_solution(2901888621912137768)
XLA Ops:
  6.6 0.7 all-gather.3.cloned.1.call-update
  7.3 0.7 all-gather.5.cloned.1.call-update
  8.2 0.3 fusion.14
  8.5 0.1 broadcast_multiply_fusion
  8.6 0.6 fusion.5
  9.3 0.2 slice_reduce_fusion.1
  9.5 0.2 slice_reduce_fusion
  9.7 0.2 copy.18
  10.1 0.5 copy-done.7
  11.2 0.1 copy.16
  11.3 0.1 broadcast_in_dim.40
  11.4 0.1 exp2.48.dec_ref
  11.5 0.2 fusion.4
  11.7 0.2 copy.19
  12.3 0.1 pad_maximum_fusion.rows_ref
  12.4 26.2 %all-gather.3.cloned.1.call-done.b_ref = bf16[128,12288]{1,0:T(8,128)(2,1)} async-done(((bf16[32,12288]{1,0:T(8,128)(2,1)}), bf16[128,12288]{1,0:T(8,128)(2,1)}) %all-gather.3.cloned.1.call-update) | async-done | bytes 3145744 | tf_op jit(solution)/shard_map/all_gather | solution.py:266
  38.6 2.8 %copy-done = bf16[12288,256]{1,0:T(8,128)(2,1)S(1)} copy-done((bf16[12288,256]{1,0:T(8,128)(2,1)S(1)}, bf16[12288,256]{1,0:T(8,128)(2,1)}, u32[]{:S(2)}) %copy-start) | copy-done | bytes 6291480
  41.3 1.9 %copy-done.1 = bf16[128,12288]{1,0:T(8,128)(2,1)S(1)} copy-done((bf16[128,12288]{1,0:T(8,128)(2,1)S(1)}, bf16[128,12288]{1,0:T(8,128)(2,1)}, u32[]{:S(2)}) %copy-start.1) | copy-done | bytes 3145752
  43.2 33.9 %band_state.1.in_ref = f32[128,256]{1,0:T(8,128)S(1)} custom-call(bf16[12288,256]{1,0:T(8,128)(2,1)S(1)} %copy-done, bf16[128,12288]{1,0:T(8,128)(2,1)S(1)} %copy-done.1, f32[16,12288]{1,0:T(8,128)S(1)} %pad_maximum_fusion.rows_ref, f32[48,256]{1,0:T(8,128)S(1)} %exp2.48.dec_ref, f32[1,256]{1,0:T(1,128)S(1)} %broadcast_in_dim.41.tot_ref), custom_call_target="tpu_custom_call" | custom-call | flops 3221225472 | bytes 9437184 | tf_op jit(solution)/shard_map/band_state/pallas_call | solution.py:101
  77.2 1.9 %copy-done.2 = bf16[128,12288]{1,0:T(8,128)(2,1)S(1)} copy-done((bf16[128,12288]{1,0:T(8,128)(2,1)S(1)}, bf16[128,12288]{1,0:T(8,128)(2,1)}, u32[]{:S(2)}) %copy-start.2) | copy-done | bytes 3145752
  79.1 1.9 %copy-done.3 = bf16[128,12288]{1,0:T(8,128)(2,1)S(1)} copy-done((bf16[128,12288]{1,0:T(8,128)(2,1)S(1)}, bf16[128,12288]{1,0:T(8,128)(2,1)}, u32[]{:S(2)}) %copy-start.3) | copy-done | bytes 3145752
  81.0 43.8 %gated_scan.1 = (f32[12288,256]{1,0:T(8,128)}, f32[8,12288]{1,0:T(8,128)S(1)}) custom-call(bf16[12288,256]{1,0:T(8,128)(2,1)} %x_ref.3, bf16[12288,256]{1,0:T(8,128)(2,1)} %g_ref.1, bf16[128,12288]{1,0:T(8,128)(2,1)S(1)} %copy-done.2, bf16[128,12288]{1,0:T(8,128)(2,1)S(1)} %copy-done.3, f32[16,12288]{1,0:T(8,128)S(1)} %pad_maximum_fusion.rows_ref, ...), custom_call_target="tpu_custom_call" | custom-call | flops 9663676416 | bytes 31457280 | tf_op jit(solution)/shard_map/gated_scan/pallas_call | solution.py:215
  124.8 10.8 %psum.7 = f32[12288]{0:T(1024)S(1)} all-reduce(f32[12288]{0:T(1024)S(1)} %bitcast.54), channel_id=1, replica_groups=mesh['seq'=8,'chan'=4] {'chan'}, use_global_device_ids=true, to_apply=%region_1.2 | all-reduce | flops 12288 | bytes 98304 | tf_op jit(solution)/shard_map/psum | solution.py:312
  135.6 8.6 %multiply_convert_fusion = bf16[12288,256]{1,0:T(8,128)(2,1)} fusion(f32[12288,256]{1,0:T(8,128)} %get-tuple-element.7, f32[256]{0:T(256)S(1)} %copy-done.5, f32[12288]{0:T(1024)S(1)} %add_rsqrt_fusion), kind=kLoop, calls=%fused_computation | loop fusion | flops 9437184 | bytes 18924544 | tf_op jit(solution)/shard_map/convert_element_type | solution.py:314
  (48 shorter events, 1.2 us)
Async XLA Ops:
  6.5 1.5 %copy-start.9 = (f32[4]{0:T(128)S(1)}, f32[4]{0:T(128)}, u32[]{:S(2)}) copy-start(f32[4]{0:T(128)} %param.16) | copy-start | bytes 52
  6.5 1.5 %copy-start.6 = (s32[24,2]{0,1:T(2,128)S(1)}, s32[24,2]{0,1:T(2,128)}, u32[]{:S(2)}) copy-start(s32[24,2]{0,1:T(2,128)} %param.19) | copy-start | bytes 580
  6.5 1.7 %copy-start.8 = (f32[4]{0:T(128)S(1)}, f32[4]{0:T(128)}, u32[]{:S(2)}) copy-start(f32[4]{0:T(128)} %param.15) | copy-start | bytes 52
  6.5 1.7 %copy-start.4 = (f32[12288,4]{0,1:T(4,128)S(1)}, f32[12288,4]{0,1:T(4,128)}, u32[]{:S(2)}) copy-start(f32[12288,4]{0,1:T(4,128)} %param.14) | copy-start | bytes 589828
  6.5 32.0 %all-gather.3.cloned.1.call-start = ((), (), s32[]{:S(2)}) async-start(), calls=%async_computation | async-start | bytes 3932160 | tf_op jit(solution)/shard_map/all_gather | solution.py:266
  7.3 69.9 %all-gather.5.cloned.1.call-start = ((), (), s32[]{:S(2)}) async-start(), calls=%async_computation.1 | async-start | bytes 3932160 | tf_op jit(solution)/shard_map/all_gather | solution.py:267
  9.9 0.7 copy-start.7
  38.6 2.8 %copy-start = (bf16[12288,256]{1,0:T(8,128)(2,1)S(1)}, bf16[12288,256]{1,0:T(8,128)(2,1)}, u32[]{:S(2)}) copy-start(bf16[12288,256]{1,0:T(8,128)(2,1)} %x_ref.3) | copy-start | bytes 18874372
  41.3 1.9 %copy-start.1 = (bf16[128,12288]{1,0:T(8,128)(2,1)S(1)}, bf16[128,12288]{1,0:T(8,128)(2,1)}, u32[]{:S(2)}) copy-start(bf16[128,12288]{1,0:T(8,128)(2,1)} %all-gather.3.cloned.1.call-done.b_ref) | copy-start | bytes 9437188
  77.2 1.9 %copy-start.2 = (bf16[128,12288]{1,0:T(8,128)(2,1)S(1)}, bf16[128,12288]{1,0:T(8,128)(2,1)}, u32[]{:S(2)}) copy-start(bf16[128,12288]{1,0:T(8,128)(2,1)} %all-gather.3.cloned.1.call-done.b_ref) | copy-start | bytes 9437188
  79.1 1.9 %copy-start.3 = (bf16[128,12288]{1,0:T(8,128)(2,1)S(1)}, bf16[128,12288]{1,0:T(8,128)(2,1)}, u32[]{:S(2)}) copy-start(bf16[128,12288]{1,0:T(8,128)(2,1)} %all-gather.5.cloned.1.call-done.c_ref) | copy-start | bytes 9437188
  81.0 54.6 %copy-start.5 = (f32[256]{0:T(256)S(1)}, f32[256]{0:T(256)}, u32[]{:S(2)}) copy-start(f32[256]{0:T(256)} %param.18) | copy-start | bytes 3076
Sparse Core Ops, SparseCore 0:
  8.9 29.6 all-gather.2
  40.1 28.4 all-gather.4
where the time goes:
time: 151 us
  Pallas kernels  77.7 us (51%)
  waiting for transfers between devices  27.6 us (18%)
  between operations  13.7 us (9%)
  blocking collectives  10.8 us (7%)
  local copies, waits for them, and re-layouts  10.6 us (7%)
  other arithmetic  9.99 us (7%)
    pallas_call x1, Pallas kernels, gated_scan(): pl.pallas_call(functools.partial(scan_kernel, heads, width), grid=(tokens...  43.8 us
    pallas_call x1, Pallas kernels, band_state(): pl.pallas_call(functools.partial(state_kernel, axis, n, heads, width), gr...  33.9 us
    all_gather x1, waiting for transfers between devices, per_device(): b_all = lax.all_gather(input_map.T, 'chan', axis=0, tiled=True)  26.2 us
    psum x1, blocking collectives, per_device(): square_sum = lax.psum(squares[0], 'chan')  10.8 us
    unnamed x25, local copies, waits for them, and re-layouts  9.55 us
    convert_element_type x1, other arithmetic, per_device(): return (gated * scale[:, None] * norm_gain).astype(BF16)  8.62 us
  transfers between devices with their start and end apart: 2, of which 1 were waited for; matrix products, arithmetic and copies ran while one was open for 2% of the time, Pallas kernels for 22%

commit v1 on v0

--- a/solution.py
+++ b/solution.py
@@ -39,7 +39,7 @@
 
 def state_kernel(
     axis, n, heads, width, x_ref, b_ref, rows_ref, dec_ref, tot_ref, out_ref,
-    xb, st, slots, send_sem, recv_sem,
+    xb, st, sent, slots, send_sem, recv_sem,
 ):
     step = pl.program_id(0)
     last = pl.num_programs(0) - 1
@@ -53,10 +53,16 @@
             pl.semaphore_signal(barrier, inc=1, device_id={axis: lax.rem(me + k, n)})
         xb[...] = jnp.zeros_like(xb)
         st[...] = jnp.zeros_like(st)
-        st[states : states + PAD, :] = jnp.broadcast_to(tot_ref[...], (PAD, st.shape[1]))
+        tot = jnp.broadcast_to(tot_ref[...], (2 * PAD, st.shape[1]))
+        first = tot.astype(BF16).astype(F32)
+        second = (tot - first).astype(BF16).astype(F32)
+        third = tot - first - second
+        row = lax.broadcasted_iota(jnp.int32, tot.shape, 0)
+        parts = jnp.where(row == 0, first, jnp.where(row == 1, second, third))
+        sent[states : states + 2 * PAD, :] = parts.astype(BF16)
 
     chunks = x_ref.shape[0] // Q
-    state = st[0:states, :]
+    state = st[...]
     for c in range(chunks):
         at = slice(c * Q, (c + 1) * Q)
         put_heads(xb.at[c % 2], x_ref[at, :], heads, width)
@@ -67,16 +73,17 @@
         )
         fresh = jnp.dot(bs, xb[c % 2], preferred_element_type=F32)
         state = state * dec_ref[pl.ds(step * chunks + c, 1), :] + fresh
-    st[0:states, :] = state
+    st[...] = state
 
     @pl.when(step == last)
     def _():
+        sent[0:states, :] = state.astype(BF16)
         barrier = pltpu.get_barrier_semaphore()
         pl.semaphore_wait(barrier, n - 1)
         copies = []
         for k in range(1, n):
             copy = pltpu.make_async_remote_copy(
-                src_ref=st,
+                src_ref=sent,
                 dst_ref=slots.at[k],
                 send_sem=send_sem.at[k],
                 recv_sem=recv_sem.at[k],
@@ -89,8 +96,10 @@
         total = jnp.zeros((states, st.shape[1]), F32)
         for k in range(n - 1, 0, -1):
             live = (k <= me).astype(F32)
-            got = slots[k]
-            total = total * jnp.exp2(got[states : states + 1, :] * live) + got[0:states, :] * live
+            got = slots[k, 0:states, :].astype(F32)
+            parts = slots[k, states : states + 2 * PAD, :].astype(F32)
+            fall = parts[0:1, :] + parts[1:2, :] + parts[2:3, :]
+            total = total * jnp.exp2(fall * live) + got * live
         out_ref[...] = total
 
 
@@ -112,13 +121,14 @@
         out_shape=jax.ShapeDtypeStruct((states, lanes), F32),
         scratch_shapes=[
             pltpu.VMEM((2, heads * Q, lanes), BF16),
-            pltpu.VMEM((states + PAD, lanes), F32),
-            pltpu.VMEM((n, states + PAD, lanes), F32),
+            pltpu.VMEM((states, lanes), F32),
+            pltpu.VMEM((states + 2 * PAD, lanes), BF16),
+            pltpu.VMEM((n, states + 2 * PAD, lanes), BF16),
             pltpu.SemaphoreType.DMA((n,)),
             pltpu.SemaphoreType.DMA((n,)),
         ],
         compiler_params=pltpu.CompilerParams(
-            collective_id=1, has_side_effects=True, vmem_limit_bytes=40 * 2**20
+            collective_id=1, has_side_effects=True, vmem_limit_bytes=60 * 2**20
         ),
         cost_estimate=pl.CostEstimate(
             flops=2 * tokens * heads * states * lanes,
@@ -130,15 +140,20 @@
 
 
 def scan_kernel(
-    heads, width, x_ref, g_ref, b_ref, c_ref, rows_ref, cols_ref, sel_ref, dec_ref, in_ref,
-    skip_ref, out_ref, sq_ref, lhs, xb, st,
+    axis, n, heads, width, x_ref, g_ref, b_ref, c_ref, rows_ref, cols_ref, sel_ref, dec_ref, in_ref,
+    skip_ref, out_ref, sq_ref, lhs, xb, st, mine, slots, send_sem, recv_sem,
 ):
     step = pl.program_id(0)
     states = b_ref.shape[0]
     lanes = x_ref.shape[1]
 
+    me = lax.axis_index(axis)
+
     @pl.when(step == 0)
     def _():
+        barrier = pltpu.get_barrier_semaphore()
+        for k in range(1, n):
+            pl.semaphore_signal(barrier, inc=1, device_id={axis: lax.rem(me + k, n)})
         xb[...] = jnp.zeros_like(xb)
         lhs[...] = jnp.zeros_like(lhs)
         st[...] = in_ref[...]
@@ -197,23 +212,48 @@
         square = gated * gated
         sq_high = square.astype(BF16)
         sq_low = (square - sq_high.astype(F32)).astype(BF16)
-        sq_ref[:, at] = lax.dot_general(
+        sums = lax.dot_general(
             ones,
             jnp.concatenate([sq_high, sq_low], axis=1),
             (((1,), (1,)), ((), ())),
             preferred_element_type=F32,
         )
+        mine[pl.ds(step * chunks + c, 1), :] = sums[0:1, :]
         state = state * dec_ref[pl.ds(step * chunks + c, 1), :] + both[Q : Q + states]
     st[...] = state
 
-
-def gated_scan(x, g, b_all, c_all, rows, cols, sel, dec, incoming, skip, heads, width):
+    @pl.when(step == pl.num_programs(0) - 1)
+    def _():
+        barrier = pltpu.get_barrier_semaphore()
+        pl.semaphore_wait(barrier, n - 1)
+        copies = []
+        for k in range(1, n):
+            copy = pltpu.make_async_remote_copy(
+                src_ref=mine,
+                dst_ref=slots.at[k],
+                send_sem=send_sem.at[k],
+                recv_sem=recv_sem.at[k],
+                device_id={axis: lax.rem(me + k, n)},
+            )
+            copy.start()
+            copies.append(copy)
+        for copy in copies:
+            copy.wait()
+        total = mine[...]
+        for k in range(1, n):
+            total = total + slots[k]
+        sq_ref[...] = total
+
+
+def gated_scan(
+    x, g, b_all, c_all, rows, cols, sel, dec, incoming, skip, axis, n, heads, width
+):
     tokens, lanes = x.shape
     states = b_all.shape[0]
     block = 1024 if tokens % 1024 == 0 else ROW
     whole = lambda a: pl.BlockSpec(a.shape, lambda i: (0, 0))
     return pl.pallas_call(
-        functools.partial(scan_kernel, heads, width),
+        functools.partial(scan_kernel, axis, n, heads, width),
         grid=(tokens // block,),
         in_specs=[
             pl.BlockSpec((block, lanes), lambda i: (i, 0)),
@@ -229,18 +269,24 @@
         ],
         out_specs=[
             pl.BlockSpec((block, lanes), lambda i: (i, 0)),
-            pl.BlockSpec((PAD, block), lambda i: (0, i)),
+            pl.BlockSpec((tokens // Q, Q), lambda i: (0, 0)),
         ],
         out_shape=[
             jax.ShapeDtypeStruct((tokens, lanes), F32),
-            jax.ShapeDtypeStruct((PAD, tokens), F32),
+            jax.ShapeDtypeStruct((tokens // Q, Q), F32),
         ],
         scratch_shapes=[
             pltpu.VMEM((2, Q + states, heads * Q), BF16),
             pltpu.VMEM((2, heads * Q, lanes), BF16),
             pltpu.VMEM((states, lanes), F32),
-        ],
-        compiler_params=pltpu.CompilerParams(vmem_limit_bytes=40 * 2**20),
+            pltpu.VMEM((tokens // Q, Q), F32),
+            pltpu.VMEM((n, tokens // Q, Q), F32),
+            pltpu.SemaphoreType.DMA((n,)),
+            pltpu.SemaphoreType.DMA((n,)),
+        ],
+        compiler_params=pltpu.CompilerParams(
+            collective_id=2, has_side_effects=True, vmem_limit_bytes=60 * 2**20
+        ),
         cost_estimate=pl.CostEstimate(
             flops=2 * tokens * heads * (Q + states) * lanes,
             bytes_accessed=tokens * (lanes * 2 + states) * 4,
@@ -252,6 +298,7 @@
 
 def per_device(
     seq_size,
+    chan_size,
     features,
     gate_input,
     input_map,
@@ -307,10 +354,10 @@
     )
     skip = jnp.repeat(skip_gain, width)[None, :]
     gated, squares = gated_scan(
-        features, gate_input, b_all, c_all, rows, cols, sel, dec, incoming, skip, heads, width
-    )
-    square_sum = lax.psum(squares[0], "chan")
-    scale = lax.rsqrt(square_sum / D + EPS)
+        features, gate_input, b_all, c_all, rows, cols, sel, dec, incoming, skip,
+        "chan", chan_size, heads, width,
+    )
+    scale = lax.rsqrt(squares.reshape(tokens) / D + EPS)
     return (gated * scale[:, None] * norm_gain).astype(BF16)
 
 
@@ -328,7 +375,7 @@
         P("seq", None),
     )
     return jax.shard_map(
-        functools.partial(per_device, mesh.shape["seq"]),
+        functools.partial(per_device, mesh.shape["seq"], mesh.shape["chan"]),
         mesh=mesh,
         in_specs=in_specs,
         out_specs=P("seq", "chan"),

time: 151 us -> 134 us (0.89); the launches traced: 151 us -> 132 us
  blocking collectives: 10.8 us -> 0 us
  local copies, waits for them, and re-layouts: 10.6 us -> 3.93 us
  Pallas kernels: 77.7 us -> 72.6 us
  other arithmetic: 9.99 us -> 12.4 us
    psum x1 -> x0, blocking collectives: 10.8 us -> none  [per_device(): square_sum = lax.psum(squares[0], 'chan')]
    pallas_call x1, Pallas kernels: 33.9 us -> 25.2 us  [band_state(): pl.pallas_call(functools.partial(state_kernel, axis, n, heads, width), gr...]
    unnamed x25 -> x20, local copies, waits for them, and re-layouts: 9.55 us -> 1.14 us
    all_gather x1, waiting for transfers between devices: 0.02 us -> 4.91 us  [per_device(): c_all = lax.all_gather(output_map.T, 'chan', axis=0, tiled=True)]
    pallas_call x1, Pallas kernels: 43.8 us -> 47.4 us  [gated_scan(): pl.pallas_call(functools.partial(scan_kernel, axis, n, heads, width), gri...]
    all_gather x1, waiting for transfers between devices: 26.2 us -> 22.9 us  [per_device(): b_all = lax.all_gather(input_map.T, 'chan', axis=0, tiled=True)]
  transfers between devices with their start and end apart: 2 -> 2, of which waited for: 1 -> 2; matrix products, arithmetic and copies ran while one was open for 2% -> 5% of each run, Pallas kernels for 22% -> 19%
where the time goes in v1:
time: 134 us; the launch traced here: 132 us
  Pallas kernels  72.6 us (54%)
  waiting for transfers between devices  29.1 us (22%)
  between operations  13.7 us (10%)
  other arithmetic  12.4 us (9%)
  local copies, waits for them, and re-layouts  3.93 us (3%)
    pallas_call x1, Pallas kernels, gated_scan(): pl.pallas_call(functools.partial(scan_kernel, axis, n, heads, width), gri...  47.4 us
    pallas_call x1, Pallas kernels, band_state(): pl.pallas_call(functools.partial(state_kernel, axis, n, heads, width), gr...  25.2 us
    all_gather x1, waiting for transfers between devices, per_device(): b_all = lax.all_gather(input_map.T, 'chan', axis=0, tiled=True)  22.9 us
    convert_element_type x1, other arithmetic, per_device(): return (gated * scale[:, None] * norm_gain).astype(BF16)  8.61 us
    all_gather x1, waiting for transfers between devices, per_device(): c_all = lax.all_gather(output_map.T, 'chan', axis=0, tiled=True)  4.91 us
  transfers between devices with their start and end apart: 2, of which 2 were waited for; matrix products, arithmetic and copies ran while one was open for 5% of the time, Pallas kernels for 19%

profile of v1, /device:TPU:12, one launch (start us, length us, event | category | flops | bytes accessed | tf_op | source)
XLA Modules:
  0.0 132.4 jit_solution(1408212772202372914)
XLA Ops:
  6.6 0.7 all-gather.3.cloned.1.call-update
  7.3 0.7 all-gather.5.cloned.1.call-update
  8.2 0.3 fusion.14
  8.5 0.1 broadcast_multiply_fusion
  8.6 0.6 fusion.5
  9.3 0.2 slice_reduce_fusion.1
  9.5 0.2 slice_reduce_fusion
  9.7 0.2 copy.18
  10.1 0.5 copy-done.4
  10.7 0.6 broadcast_in_dim_reshape.3.skip_ref
  11.6 0.6 broadcast_in_dim.41.tot_ref
  12.3 0.1 copy.16
  12.4 0.1 broadcast_in_dim.40
  12.5 0.7 exp2.48.dec_ref
  13.2 0.2 fusion.4
  13.4 0.2 copy.19
  13.9 0.6 maximum_maximum_fusion.sel_ref
  14.6 1.1 pad_maximum_fusion.rows_ref
  15.7 22.9 %all-gather.3.cloned.1.call-done.b_ref = bf16[128,12288]{1,0:T(8,128)(2,1)} async-done(((bf16[32,12288]{1,0:T(8,128)(2,1)}), bf16[128,12288]{1,0:T(8,128)(2,1)}) %all-gather.3.cloned.1.call-update) | async-done | bytes 3145744 | tf_op jit(solution)/shard_map/all_gather | solution.py:313
  38.6 25.2 %band_state.1.in_ref = f32[128,256]{1,0:T(8,128)} custom-call(bf16[12288,256]{1,0:T(8,128)(2,1)} %x_ref.3, bf16[128,12288]{1,0:T(8,128)(2,1)} %all-gather.3.cloned.1.call-done.b_ref, f32[16,12288]{1,0:T(8,128)} %pad_maximum_fusion.rows_ref, f32[48,256]{1,0:T(8,128)} %exp2.48.dec_ref, f32[1,256]{1,0:T(1,128)} %broadcast_in_dim.41.tot_ref), custom_call_target="tpu_custom_call" | custom-call | flops 3221225472 | bytes 9437184 | tf_op jit(solution)/shard_map/band_state/pallas_call | solution.py:110
  63.8 4.9 %all-gather.5.cloned.1.call-done.c_ref = bf16[128,12288]{1,0:T(8,128)(2,1)} async-done(((bf16[32,12288]{1,0:T(8,128)(2,1)}), bf16[128,12288]{1,0:T(8,128)(2,1)}) %all-gather.5.cloned.1.call-update) | async-done | bytes 3145744 | tf_op jit(solution)/shard_map/all_gather | solution.py:314
  68.7 47.4 %gated_scan.1 = (f32[12288,256]{1,0:T(8,128)}, f32[48,256]{1,0:T(8,128)}) custom-call(bf16[12288,256]{1,0:T(8,128)(2,1)} %x_ref.3, bf16[12288,256]{1,0:T(8,128)(2,1)} %g_ref.1, bf16[128,12288]{1,0:T(8,128)(2,1)} %all-gather.3.cloned.1.call-done.b_ref, bf16[128,12288]{1,0:T(8,128)(2,1)} %all-gather.5.cloned.1.call-done.c_ref, ...), custom_call_target="tpu_custom_call" | custom-call | flops 9663676416 | bytes 31457280 | tf_op jit(solution)/shard_map/gated_scan/pallas_call | solution.py:255
  116.1 0.8 rsqrt_bitcast_fusion
  117.0 8.6 %multiply_convert_fusion = bf16[12288,256]{1,0:T(8,128)(2,1)} fusion(f32[12288,256]{1,0:T(8,128)} %get-tuple-element.7, f32[256]{0:T(256)S(1)} %copy-done.2, f32[12288]{0:T(1024)S(1)} %bitcast.57), kind=kLoop, calls=%fused_computation | loop fusion | flops 9437184 | bytes 18924544 | tf_op jit(solution)/shard_map/convert_element_type | solution.py:361
  (41 shorter events, 1.0 us)
Async XLA Ops:
  6.5 1.5 %copy-start.6 = (f32[4]{0:T(128)S(1)}, f32[4]{0:T(128)}, u32[]{:S(2)}) copy-start(f32[4]{0:T(128)} %param.16) | copy-start | bytes 52
  6.5 1.5 %copy-start.3 = (s32[24,2]{0,1:T(2,128)S(1)}, s32[24,2]{0,1:T(2,128)}, u32[]{:S(2)}) copy-start(s32[24,2]{0,1:T(2,128)} %param.19) | copy-start | bytes 580
  6.5 1.7 %copy-start.5 = (f32[4]{0:T(128)S(1)}, f32[4]{0:T(128)}, u32[]{:S(2)}) copy-start(f32[4]{0:T(128)} %param.15) | copy-start | bytes 52
  6.5 1.7 %copy-start = (f32[12288,4]{0,1:T(4,128)S(1)}, f32[12288,4]{0,1:T(4,128)}, u32[]{:S(2)}) copy-start(f32[12288,4]{0,1:T(4,128)} %param.14) | copy-start | bytes 589828
  6.5 32.0 %all-gather.3.cloned.1.call-start = ((), (), s32[]{:S(2)}) async-start(), calls=%async_computation | async-start | bytes 3932160 | tf_op jit(solution)/shard_map/all_gather | solution.py:313
  7.3 61.5 %all-gather.5.cloned.1.call-start = ((), (), s32[]{:S(2)}) async-start(), calls=%async_computation.1 | async-start | bytes 3932160 | tf_op jit(solution)/shard_map/all_gather | solution.py:314
  9.9 0.7 copy-start.4
  14.6 49.2 %copy-start.1 = (bf16[48,12288]{1,0:T(8,128)(2,1)}, bf16[48,12288]{1,0:T(8,128)(2,1)S(1)}, u32[]{:S(2)}) copy-start(bf16[48,12288]{1,0:T(8,128)(2,1)S(1)} %broadcast_dynamic-update-slice_fusion.cols_ref) | copy-start | bytes 3538948
  63.8 53.1 %copy-start.2 = (f32[256]{0:T(256)S(1)}, f32[256]{0:T(256)}, u32[]{:S(2)}) copy-start(f32[256]{0:T(256)} %param.18) | copy-start | bytes 3076
Sparse Core Ops, SparseCore 0:
  8.9 29.6 all-gather.2
  40.1 28.5 all-gather.4
